TPU v7x, 32 devices: a whole 2x2x4 slice. The times are simulated.
32 devices in a mesh: dp: 16 (over z, y, core), sp: 2 (over x).
Axes of the slice: x: 2, y: 2, z: 4, core: 2. Of those that a mesh axis runs over, the one named last changes fastest.
Arguments:
- hidden: bfloat16 [16, 4, 128, 3584], P('dp', None, 'sp'), may hold values from -6 to 6
- segment_ids: int32 [16, 4, 128], P('dp'), may hold values from -1 to 15, as said below
- w_query: bfloat16 [3584, 3584], P(None, 'sp'), may hold values from -0.10022297 to 0.10022297
- key_matrix: bfloat16 [3584, 512], P(None, 'sp'), may hold values from -0.10022297 to 0.10022297
- value_matrix: bfloat16 [3584, 512], P(None, 'sp'), may hold values from -0.10022297 to 0.10022297
Outputs:
- mixed: bfloat16 [16, 512, 3584], P('dp', 'sp')
Inputs may be any that keep to these rules, and one draw needn't show every extreme that they name: `segment_ids`: in each outbox the live slots come first; over them the ids start at 0 and never fall, by steps of 0 or 1; empty slots hold -1. Every group has an outbox whose 128 slots are all live.
All inputs are finite; a program needn't handle non-finite values.
Results may differ from a plain program's by a relative error of at most 0.0087.
Values may be sent and summed in bfloat16 or wider, within the bound.
No kernel may reach another device: no remote copies, remote signals or barrier semaphores. Data moves between devices by JAX's collectives and lax.ppermute only.
A program may use at most 64 MiB of HBM per device.

v0:
```python
import jax
import jax.numpy as jnp
from jax import lax
from jax.sharding import PartitionSpec as P

HEAD_SIZE = 128
NSEG = 16
GROUP_SLOTS = 512
ROPE_BASE = 1000000.0


def shifted(value, axis, steps):
    count = lax.axis_size(axis)
    pairs = [(source, (source + steps) % count) for source in range(count)]
    return lax.ppermute(value, axis, pairs)


def rotate(tensor, where):
    half_width = tensor.shape[-1] // 2
    freq = ROPE_BASE ** (-(jnp.arange(half_width, dtype=jnp.float32) * 2.0 / tensor.shape[-1]))
    angle = where[:, None] * freq[None, :]
    cosine = jnp.cos(angle)[:, None, :]
    sine = jnp.sin(angle)[:, None, :]
    first = tensor[..., :half_width]
    second = tensor[..., half_width:]
    return jnp.concatenate(
        [first * cosine - second * sine, second * cosine + first * sine], axis=-1
    )


def positions(segments):
    slot_ids = jnp.arange(NSEG, dtype=jnp.int32)
    onehot = (segments[..., :, None] == slot_ids).astype(jnp.int32)
    living = (segments >= 0).astype(jnp.int32)
    below = jnp.sum(
        (segments[..., :, None] < slot_ids).astype(jnp.int32) * living[..., :, None], axis=-2
    )
    first_slot = jnp.sum(onehot * below[..., None, :], axis=-1)
    index = jnp.arange(segments.shape[-1], dtype=jnp.int32)
    return (index - first_slot).astype(jnp.float32)


def attend(queries, projected_key_rows, projected_value_rows, labels):
    total_rows = queries.shape[0]
    kv_heads = projected_key_rows.shape[1]
    queries = queries.reshape(total_rows, kv_heads, -1, queries.shape[-1])
    scores = jnp.einsum(
        "qcgd,kcd->cgqk", queries, projected_key_rows, preferred_element_type=jnp.float32
    )
    scores = scores / jnp.sqrt(jnp.float32(queries.shape[-1]))
    index = jnp.arange(total_rows, dtype=jnp.int32)
    seen = (
        (labels[:, None] == labels[None, :])
        & (labels[:, None] >= 0)
        & (index[None, :] <= index[:, None])
    )
    seen = seen | (index[:, None] == index[None, :])
    scores = jnp.where(seen, scores, -1e30)
    largest = jnp.max(scores, axis=-1, keepdims=True)
    expo = jnp.where(seen, jnp.exp(scores - largest), 0.0)
    denominator = jnp.sum(expo, axis=-1, keepdims=True)
    probs = expo.astype(jnp.bfloat16)
    summed = jnp.einsum(
        "cgqk,kcd->qcgd", probs, projected_value_rows, preferred_element_type=jnp.float32
    )
    summed = summed / jnp.transpose(denominator, (2, 0, 1, 3))
    living = (labels >= 0).astype(jnp.float32)
    return (summed.reshape(total_rows, -1) * living[:, None]).astype(jnp.bfloat16)


def local(hidden, segment_ids, w_query, key_matrix, value_matrix):
    outboxes = hidden.shape[1]
    arrivals = [(hidden[:, 0], segment_ids[:, 0])]
    for stride in range(1, outboxes):
        arrivals.append(shifted((hidden[:, stride], segment_ids[:, stride]), "dp", stride))
    tokens_in = jnp.stack([entry[0] for entry in arrivals], axis=1)
    segments = jnp.stack([entry[1] for entry in arrivals], axis=1)
    where_all = positions(segments)
    box_ids = jnp.arange(outboxes, dtype=jnp.int32)[None, :, None]
    labels = jnp.where(segments >= 0, box_ids * NSEG + segments, -1).reshape(-1)
    query_cols = w_query.shape[1]
    key_cols = key_matrix.shape[1]
    w_joined = jnp.concatenate([w_query, key_matrix, value_matrix], axis=1)
    portion = lax.all_gather(tokens_in, "sp", axis=2, tiled=True)
    width_rows = portion.shape[2]
    flat = portion.reshape(-1, portion.shape[3])
    product = jnp.dot(flat, w_joined, preferred_element_type=jnp.float32)
    where_part = where_all.reshape(-1)
    queries = rotate(
        product[:, :query_cols].reshape(flat.shape[0], -1, HEAD_SIZE), where_part
    ).astype(jnp.bfloat16)
    projected_key_rows = rotate(
        product[:, query_cols : query_cols + key_cols].reshape(flat.shape[0], -1, HEAD_SIZE),
        where_part,
    ).astype(jnp.bfloat16)
    projected_value_rows = product[:, query_cols + key_cols :].astype(jnp.bfloat16)
    joined = jnp.concatenate(
        [
            queries.reshape(flat.shape[0], -1),
            projected_key_rows.reshape(flat.shape[0], -1),
            projected_value_rows,
        ],
        axis=1,
    )
    projected = joined.reshape(1, outboxes, width_rows, -1)
    projected = projected.reshape(GROUP_SLOTS, -1)
    queries = projected[:, :query_cols].reshape(GROUP_SLOTS, -1, HEAD_SIZE)
    projected_key_rows = projected[:, query_cols : query_cols + key_cols].reshape(
        GROUP_SLOTS, -1, HEAD_SIZE
    )
    projected_value_rows = projected[:, query_cols + key_cols :].reshape(GROUP_SLOTS, -1, HEAD_SIZE)
    attended = attend(queries, projected_key_rows, projected_value_rows, labels).reshape(
        1, GROUP_SLOTS, -1
    )
    return lax.all_to_all(attended, "sp", split_axis=1, concat_axis=2, tiled=True)


def solution(mesh):
    placed = (
        P("dp", None, "sp", None),
        P("dp", None, None),
        P(None, "sp"),
        P(None, "sp"),
        P(None, "sp"),
    )
    return jax.shard_map(
        local, mesh=mesh, in_specs=placed, out_specs=P("dp", "sp", None), check_vma=False
    )
```

profile of v0, /device:TPU:0, one launch (start us, length us, event | category | flops | bytes accessed | tf_op | source)
XLA Modules:
  0.0 220.1 jit_solution(8252332415008291170)
XLA Ops:
  8.1 2.5 %collective-permute-start.2 = (bf16[1,64,3584]{2,1,0:T(8,128)(2,1)S(1)}, bf16[1,64,3584]{2,1,0:T(8,128)(2,1)S(1)}, u32[]{:S(2)}, u32[]{:S(2)}) collective-permute-start(bf16[1,64,3584]{2,1,0:T(8,128)(2,1)S(1)} %get-tuple-element.12), channel_id=1, source_target_pairs={{0,6},{2,8},{4,10},{6,12},{8,14},{10,16},{12,18},{14,20},{16,22},{... | collective-permute-start | bytes 1376264 | tf_op jit(solution)/shard_map/ppermute | solution.py:15
  12.6 7.7 %collective-permute-done.2 = bf16[1,64,3584]{2,1,0:T(8,128)(2,1)S(1)} collective-permute-done((bf16[1,64,3584]{2,1,0:T(8,128)(2,1)S(1)}, bf16[1,64,3584]{2,1,0:T(8,128)(2,1)S(1)}, u32[]{:S(2)}, u32[]{:S(2)}) %collective-permute-start.2) | collective-permute-done | bytes 458784 | tf_op jit(solution)/shard_map/ppermute | solution.py:15
  20.2 15.2 %collective-permute-done.1 = bf16[1,64,3584]{2,1,0:T(8,128)(2,1)S(1)} collective-permute-done((bf16[1,64,3584]{2,1,0:T(8,128)(2,1)S(1)}, bf16[1,64,3584]{2,1,0:T(8,128)(2,1)S(1)}, u32[]{:S(2)}, u32[]{:S(2)}) %collective-permute-start.1) | collective-permute-done | bytes 458784 | tf_op jit(solution)/shard_map/ppermute | solution.py:15
  35.4 4.6 %collective-permute-done = bf16[1,64,3584]{2,1,0:T(8,128)(2,1)S(1)} collective-permute-done((bf16[1,64,3584]{2,1,0:T(8,128)(2,1)S(1)}, bf16[1,64,3584]{2,1,0:T(8,128)(2,1)S(1)}, u32[]{:S(2)}, u32[]{:S(2)}) %collective-permute-start) | collective-permute-done | bytes 458784 | tf_op jit(solution)/shard_map/ppermute | solution.py:15
  41.7 4.6 %collective-permute-done.5 = s32[1,128]{1,0:T(1,128)S(1)} collective-permute-done((s32[1,128]{1,0:T(1,128)S(1)}, s32[1,128]{1,0:T(1,128)S(1)}, u32[]{:S(2)}, u32[]{:S(2)}) %collective-permute-start.5) | collective-permute-done | bytes 544 | tf_op jit(solution)/shard_map/ppermute | solution.py:15
  50.0 40.8 %all-gather.2.cloned.1.call-done = bf16[1,4,128,3584]{3,2,1,0:T(8,128)(2,1)} async-done(((bf16[1,4,64,3584]{3,2,1,0:T(8,128)(2,1)}), bf16[1,4,128,3584]{3,2,1,0:T(8,128)(2,1)}) %all-gather.2.cloned.1.call-update) | async-done | bytes 3670032 | tf_op jit(solution)/shard_map/all_gather | solution.py:84
  90.9 13.2 %fusion.1 = f32[512,2304]{1,0:T(8,128)S(1)} fusion(bf16[512,3584]{1,0:T(8,128)(2,1)} %bitcast.96, bf16[3584,256]{1,0:T(8,128)(2,1)S(1)} %copy-done.5, bf16[3584,256]{1,0:T(8,128)(2,1)} %param.8, bf16[3584,1792]{1,0:T(8,128)(2,1)} %param.7), kind=kOutput, calls=%fused_computation.1 | convolution fusion | flops 8505262080 | bytes 24903680 | tf_op jit(solution)/shard_map/dot_general | solution.py:87
  104.1 2.2 %slice.65 = f32[512,1792]{1,0:T(8,128)} slice(f32[512,2304]{1,0:T(8,128)S(1)} %fusion.1), slice={[0:512], [0:1792]} | slice | bytes 7340032 | tf_op jit(solution)/shard_map/slice | solution.py:90
  108.1 5.1 %copy.85 = f32[512,1792]{0,1:T(8,128)} copy(f32[512,1792]{1,0:T(8,128)} %slice.65) | data formatting | bytes 7340032 | tf_op jit(solution)/shard_map/slice | solution.py:90
  113.2 3.9 %subtract_convert_fusion = (bf16[512,14,64]{0,2,1:T(8,128)(2,1)}, bf16[512,14,64]{0,2,1:T(8,128)(2,1)}) fusion(f32[512,14,128]{0,2,1:T(8,128)} %bitcast.77, f32[512,64]{0,1:T(8,128)S(1)} %get-tuple-element.19, f32[512,64]{0,1:T(8,128)S(1)} %get-tuple-element.18), kind=kLoop, calls=%fused_computation.23 | loop fusion | flops 3670016 | bytes 5767168 | tf_op jit(solution)/shard_map/convert.3
  117.1 2.0 copy.87
  119.1 2.6 %copy.86 = bf16[512,14,64]{2,0,1:T(8,128)(2,1)} copy(bf16[512,14,64]{0,2,1:T(8,128)(2,1)} %get-tuple-element.8) | data formatting | bytes 1835008 | tf_op jit(solution)/shard_map/convert.3
  123.5 7.4 %fusion.15 = f32[2,512,512,7]{2,1,3,0:T(8,128)} fusion(bf16[512,2,7,64]{3,0,2,1:T(8,128)(2,1)S(1)} %bitcast.80, bf16[512,2,7,64]{3,0,2,1:T(8,128)(2,1)S(1)} %bitcast.81, bf16[512,2,64]{2,0,1:T(8,128)(2,1)S(1)} %get-tuple-element.15, bf16[512,2,64]{2,0,1:T(8,128)(2,1)S(1)} %get-tuple-element.14), kind=kOutput, calls=%fused_computation.18 | convolution fusion | flops 943718400 | bytes 16777216 | tf_op jit(solution)/shard_map/qcgd,kcd->cgqk/dot_general | solution.py:47
  130.8 13.6 %fusion.35 = (f32[2,7,512]{2,1,0:T(8,128)S(1)}, bf16[2,7,512,512]{2,3,1,0:T(8,128)(2,1)S(1)}) fusion(f32[2,512,512,7]{2,1,3,0:T(8,128)} %fusion.15, pred[512,512]{0,1:T(8,128)(4,1)S(1)} %copy-done.2), kind=kOutput, calls=%fused_computation.66 | output fusion | flops 29360640 | bytes 22310912 | tf_op jit(solution)/shard_map/sub | solution.py:60
  144.5 2.9 %bitcast_divide_fusion = f32[512,2,7,128]{0,3,2,1:T(8,128)} fusion(bf16[512,2,128,1]{0,2,3,1:T(8,128)(2,1)S(1)} %bitcast.88, bf16[2,7,512,512]{2,3,1,0:T(8,128)(2,1)S(1)} %get-tuple-element.26, f32[512,2,7]{0,2,1:T(8,128)S(1)} %bitcast.97), kind=kOutput, calls=%fused_computation.15 | convolution fusion | flops 940441600 | bytes 11300864 | tf_op jit(solution)/shard_map/cgqk,kcd->qcgd/dot_general | solution.py:63
  147.5 5.1 %copy.90 = f32[1,512,1792]{2,1,0:T(8,128)} copy(f32[1,512,1792]{1,2,0:T(8,128)} %bitcast.84) | data formatting | bytes 7340032 | tf_op jit(solution)/shard_map/reshape | solution.py:68
  152.6 2.3 %multiply_convert_fusion = bf16[1,512,1792]{2,1,0:T(8,128)(2,1)S(1)} fusion(f32[1,512,1792]{2,1,0:T(8,128)} %copy.90, f32[512]{0:T(512)S(1)} %get-tuple-element.5), kind=kLoop, calls=%fused_computation.16 | loop fusion | flops 1835008 | bytes 5507072 | tf_op jit(solution)/shard_map/convert_element_type | solution.py:68
  154.9 4.6 %copy.106 = bf16[1,512,1792]{2,0,1:T(2,128)(2,1)} copy(bf16[1,512,1792]{2,1,0:T(8,128)(2,1)S(1)} %multiply_convert_fusion) | data formatting | bytes 3670016 | tf_op jit(solution)/shard_map/convert_element_type | solution.py:68
  160.0 13.1 %reduce.2 = bf16[512,1792]{1,0:T(8,128)(2,1)} reduce(bf16[512,1,1792]{2,1,0:T(2,128)(2,1)} %bitcast.78, bf16[]{:T(256)} %broadcast.216), dimensions={1}, to_apply=%bitcast.76.reduce_sub_computation | reduce | bytes 3670018
  174.8 25.5 %all_to_all.18 = bf16[2,2,229376]{2,1,0:T(2,128)(2,1)} all-to-all(bf16[2,2,229376]{2,1,0:T(2,128)(2,1)S(1)} %reshape.315), channel_id=1, replica_groups=mesh['dp'=16,'sp'=2] {'sp'}, dimensions={0} | all-to-all | bytes 3670016 | tf_op jit(solution)/shard_map/all_to_all | solution.py:115
  200.3 4.0 %reshape.316 = bf16[512,1,1792]{2,1,0:T(2,128)(2,1)} reshape(bf16[2,2,229376]{2,1,0:T(2,128)(2,1)} %all_to_all.18) | data formatting | bytes 3670016
  204.3 3.5 %copy.98 = bf16[1,512,1792]{2,1,0:T(8,128)(2,1)} copy(bf16[1,512,1792]{2,0,1:T(2,128)(2,1)} %bitcast.79) | data formatting | bytes 3670016
  207.8 2.8 %copy.92 = bf16[1,256,2,1792]{1,3,2,0:T(8,128)(2,1)S(1)} copy(bf16[1,256,2,1792]{3,1,2,0:T(8,128)(2,1)} %bitcast.83) | data formatting | bytes 3670016 | tf_op jit(solution)/shard_map/all_to_all | solution.py:115
  210.6 2.6 %copy.93 = bf16[1,256,3584]{2,1,0:T(8,128)(2,1)} copy(bf16[1,256,3584]{1,2,0:T(8,128)(2,1)S(1)} %bitcast.82) | data formatting | bytes 3670016 | tf_op jit(solution)/shard_map/all_to_all | solution.py:115
  (46 shorter events, 14.7 us)
Async XLA Ops:
  6.5 84.3 %all-gather.2.cloned.1.call-start = ((), (), s32[]{:S(2)}) async-start(), calls=%async_computation.1 | async-start | bytes 5505024 | tf_op jit(solution)/shard_map/all_gather | solution.py:84
  8.1 33.4 %copy-start.4 = (s32[1,4,128]{2,1,0:T(4,128)S(1)}, s32[1,4,128]{2,1,0:T(4,128)}, u32[]{:S(2)}) copy-start(s32[1,4,128]{2,1,0:T(4,128)} %param.6) | copy-start | bytes 6148
  8.1 82.8 %copy-start.5 = (bf16[3584,256]{1,0:T(8,128)(2,1)S(1)}, bf16[3584,256]{1,0:T(8,128)(2,1)}, u32[]{:S(2)}) copy-start(bf16[3584,256]{1,0:T(8,128)(2,1)} %param.9) | copy-start | bytes 5505028
  8.1 12.1 %collective-permute-start.2 = (bf16[1,64,3584]{2,1,0:T(8,128)(2,1)S(1)}, bf16[1,64,3584]{2,1,0:T(8,128)(2,1)S(1)}, u32[]{:S(2)}, u32[]{:S(2)}) collective-permute-start(bf16[1,64,3584]{2,1,0:T(8,128)(2,1)S(1)} %get-tuple-element.12), channel_id=1, source_target_pairs={{0,6},{2,8},{4,10},{6,12},{8,14},{10,16},{12,18},{14,20},{16,22},{... | collective-permute-start | bytes 1376264 | tf_op jit(solution)/shard_map/ppermute | solution.py:15
  10.6 24.8 %collective-permute-start.1 = (bf16[1,64,3584]{2,1,0:T(8,128)(2,1)S(1)}, bf16[1,64,3584]{2,1,0:T(8,128)(2,1)S(1)}, u32[]{:S(2)}, u32[]{:S(2)}) collective-permute-start(bf16[1,64,3584]{2,1,0:T(8,128)(2,1)S(1)} %get-tuple-element.13), channel_id=1, source_target_pairs={{0,4},{2,6},{4,8},{6,10},{8,12},{10,14},{12,16},{14,18},{16,20},{1... | collective-permute-start | bytes 1376264 | tf_op jit(solution)/shard_map/ppermute | solution.py:15
  12.1 27.8 %collective-permute-start = (bf16[1,64,3584]{2,1,0:T(8,128)(2,1)S(1)}, bf16[1,64,3584]{2,1,0:T(8,128)(2,1)S(1)}, u32[]{:S(2)}, u32[]{:S(2)}) collective-permute-start(bf16[1,64,3584]{2,1,0:T(8,128)(2,1)S(1)} %get-tuple-element.11), channel_id=1, source_target_pairs={{0,2},{2,4},{4,6},{6,8},{8,10},{10,12},{12,14},{14,16},{16,18},{18... | collective-permute-start | bytes 1376264 | tf_op jit(solution)/shard_map/ppermute | solution.py:15
  41.5 4.8 %collective-permute-start.5 = (s32[1,128]{1,0:T(1,128)S(1)}, s32[1,128]{1,0:T(1,128)S(1)}, u32[]{:S(2)}, u32[]{:S(2)}) collective-permute-start(s32[1,128]{1,0:T(1,128)S(1)} %get-tuple-element.23), channel_id=1, source_target_pairs={{0,6},{2,8},{4,10},{6,12},{8,14},{10,16},{12,18},{14,20},{16,22},{... | collective-permute-start | bytes 1544 | tf_op jit(solution)/shard_map/ppermute | solution.py:15
  41.5 6.3 %collective-permute-start.4 = (s32[1,128]{1,0:T(1,128)S(1)}, s32[1,128]{1,0:T(1,128)S(1)}, u32[]{:S(2)}, u32[]{:S(2)}) collective-permute-start(s32[1,128]{1,0:T(1,128)S(1)} %get-tuple-element.24), channel_id=1, source_target_pairs={{0,4},{2,6},{4,8},{6,10},{8,12},{10,14},{12,16},{14,18},{16,20},{1... | collective-permute-start | bytes 1544 | tf_op jit(solution)/shard_map/ppermute | solution.py:15
  41.6 6.3 %collective-permute-start.3 = (s32[1,128]{1,0:T(1,128)S(1)}, s32[1,128]{1,0:T(1,128)S(1)}, u32[]{:S(2)}, u32[]{:S(2)}) collective-permute-start(s32[1,128]{1,0:T(1,128)S(1)} %get-tuple-element.22), channel_id=1, source_target_pairs={{0,2},{2,4},{4,6},{6,8},{8,10},{10,12},{12,14},{14,16},{16,18},{18... | collective-permute-start | bytes 1544 | tf_op jit(solution)/shard_map/ppermute | solution.py:15
  104.1 3.2 %copy-start.1 = (f32[512,2304]{1,0:T(8,128)}, f32[512,2304]{1,0:T(8,128)S(1)}, u32[]{:S(2)}) copy-start(f32[512,2304]{1,0:T(8,128)S(1)} %fusion.1) | copy-start | bytes 14155780
  117.1 4.5 %slice-start = ((f32[512,2304]{1,0:T(8,128)}), f32[512,256]{1,0:T(8,128)S(1)}, s32[]{:S(2)}) async-start(f32[512,2304]{1,0:T(8,128)} %copy-done.1), calls=%async_computation.2 | async-start | bytes 1048576 | tf_op jit(solution)/shard_map/slice | solution.py:93
  122.0 1.5 copy-start
  123.5 7.4 %copy-start.2 = (pred[512,512]{0,1:T(8,128)(4,1)S(1)}, pred[512,512]{0,1:T(8,128)(4,1)}, u32[]{:S(2)}) copy-start(pred[512,512]{0,1:T(8,128)(4,1)} %fusion.20) | copy-start | bytes 786436
  130.8 13.7 %copy-start.3 = (bf16[512,256]{0,1:T(8,128)(2,1)S(1)}, bf16[512,256]{0,1:T(8,128)(2,1)}, u32[]{:S(2)}) copy-start(bf16[512,256]{0,1:T(8,128)(2,1)} %copy.97) | copy-start | bytes 786436
Sparse Core Ops, SparseCore 0:
  41.6 49.2 all-gather.1
where the time goes:
time: 221 us; the launch traced here: 220 us
  waiting for transfers between devices  74.4 us (34%)
  local copies, waits for them, and re-layouts  42.1 us (19%)
  other arithmetic  36.4 us (16%)
  blocking collectives  25.5 us (12%)
  matrix products  23.5 us (11%)
  between operations  13.6 us (6%)
  starting transfers between devices  4.64 us (2%)
    all_gather x1, waiting for transfers between devices, local(): portion = lax.all_gather(tokens_in, 'sp', axis=2, tiled=True)  40.8 us
    ppermute x6, waiting for transfers between devices, shifted(): return lax.ppermute(value, axis, pairs)  33.5 us
    all_to_all x1, blocking collectives, local(): lax.all_to_all(attended, 'sp', split_axis=1, concat_axis=2, tiled=True)  25.5 us
    sub x1, other arithmetic, attend(): expo = jnp.where(seen, jnp.exp(scores - largest), 0.0)  13.6 us
    dot_general x1, matrix products, local(): product = jnp.dot(flat, w_joined, preferred_element_type=jnp.float32)  13.2 us
    unnamed x1, other arithmetic  13.1 us
    unnamed x16, local copies, waits for them, and re-layouts  11.4 us
    dot_general x1, matrix products, attend(): jnp.einsum('qcgd,kcd->cgqk', queries, projected_key_rows, preferred_eleme...  7.37 us
  transfers between devices with their start and end apart: 7, of which 6 were waited for; matrix products, arithmetic and copies ran while one was open for 1% of the time, Pallas kernels for 0%

commit v1 on v0

--- a/solution.py
+++ b/solution.py
@@ -7,6 +7,13 @@
 NSEG = 16
 GROUP_SLOTS = 512
 ROPE_BASE = 1000000.0
+
+
+def swap_blocks(x, axis, split, join):
+    size = lax.axis_size(axis)
+    tiles = jnp.stack(jnp.split(x, size, axis=split), axis=0)
+    tiles = lax.all_to_all(tiles, axis, split_axis=0, concat_axis=0)
+    return jnp.concatenate(tiles, axis=join)
 
 
 def shifted(value, axis, steps):
@@ -112,7 +119,7 @@
     attended = attend(queries, projected_key_rows, projected_value_rows, labels).reshape(
         1, GROUP_SLOTS, -1
     )
-    return lax.all_to_all(attended, "sp", split_axis=1, concat_axis=2, tiled=True)
+    return swap_blocks(attended, "sp", 1, 2)
 
 
 def solution(mesh):

time: 221 us -> 181 us (0.82)
  local copies, waits for them, and re-layouts: 42.1 us -> 18.6 us
  other arithmetic: 36.4 us -> 22.5 us
  waiting for transfers between devices: 74.4 us -> 68.1 us
  starting transfers between devices: 4.64 us -> 9.7 us
    unnamed x1 -> x0, other arithmetic: 13.1 us -> none
    unnamed x16 -> x8, local copies, waits for them, and re-layouts: 11.4 us -> 0.02 us
    ppermute x6, waiting for transfers between devices: 33.5 us -> 27.8 us  [shifted(): return lax.ppermute(value, axis, pairs)]
    all_to_all x2 -> x0, local copies, waits for them, and re-layouts: 5.36 us -> none  [local(): lax.all_to_all(attended, 'sp', split_axis=1, concat_axis=2, tiled=True)]
    ppermute x6, starting transfers between devices: 4.63 us -> 9.7 us  [shifted(): return lax.ppermute(value, axis, pairs)]
    convert_element_type x1 -> x0, local copies, waits for them, and re-layouts: 4.64 us -> none  [attend(): (summed.reshape(total_rows, -1) * living[:, None]).astype(jnp.bfloat16)]
    reshape x1, local copies, waits for them, and re-layouts: 5.12 us -> 2.55 us  [swap_blocks(): return jnp.concatenate(tiles, axis=join)]
    another operation x2 -> x3, other arithmetic: 4.03 us -> 5 us
  transfers between devices with their start and end apart: 7 -> 7, of which waited for: 6 -> 7; matrix products, arithmetic and copies ran while one was open for 1% -> 2% of each run, Pallas kernels for 0% -> 0%
where the time goes in v1:
time: 181 us; the launch traced here: 180 us
  waiting for transfers between devices  68.1 us (38%)
  blocking collectives  24.7 us (14%)
  matrix products  23.2 us (13%)
  other arithmetic  22.5 us (12%)
  local copies, waits for them, and re-layouts  18.6 us (10%)
  between operations  13.6 us (8%)
  starting transfers between devices  9.7 us (5%)
    all_gather x1, waiting for transfers between devices, local(): portion = lax.all_gather(tokens_in, 'sp', axis=2, tiled=True)  40.4 us
    ppermute x6, waiting for transfers between devices, shifted(): return lax.ppermute(value, axis, pairs)  27.8 us
    all_to_all x1, blocking collectives, swap_blocks(): tiles = lax.all_to_all(tiles, axis, split_axis=0, concat_axis=0)  24.7 us
    sub x1, other arithmetic, attend(): expo = jnp.where(seen, jnp.exp(scores - largest), 0.0)  13.6 us
    dot_general x1, matrix products, local(): product = jnp.dot(flat, w_joined, preferred_element_type=jnp.float32)  13.2 us
    ppermute x6, starting transfers between devices, shifted(): return lax.ppermute(value, axis, pairs)  9.7 us
    dot_general x1, matrix products, attend(): jnp.einsum('qcgd,kcd->cgqk', queries, projected_key_rows, preferred_eleme...  8.9 us
    slice x2, local copies, waits for them, and re-layouts, local(): product[:, :query_cols].reshape(flat.shape[0], -1, HEAD_SIZE)  7.18 us
  transfers between devices with their start and end apart: 7, of which 7 were waited for; matrix products, arithmetic and copies ran while one was open for 2% of the time, Pallas kernels for 0%

profile of v1, /device:TPU:0, one launch (start us, length us, event | category | flops | bytes accessed | tf_op | source)
XLA Modules:
  0.0 180.3 jit_solution(2797308720457104253)
XLA Ops:
  6.5 1.6 fusion.32
  8.7 3.7 %collective-permute-start.2 = (bf16[1,64,3584]{2,1,0:T(8,128)(2,1)S(1)}, bf16[1,64,3584]{2,1,0:T(8,128)(2,1)S(1)}, u32[]{:S(2)}, u32[]{:S(2)}) collective-permute-start(bf16[1,64,3584]{2,1,0:T(8,128)(2,1)S(1)} %get-tuple-element.14), channel_id=1, source_target_pairs={{0,6},{2,8},{4,10},{6,12},{8,14},{10,16},{12,18},{14,20},{16,22},{... | collective-permute-start | bytes 1376264 | tf_op jit(solution)/shard_map/ppermute | solution.py:22
  12.4 1.5 collective-permute-start.1
  13.9 8.5 %collective-permute-done = bf16[1,64,3584]{2,1,0:T(8,128)(2,1)S(1)} collective-permute-done((bf16[1,64,3584]{2,1,0:T(8,128)(2,1)S(1)}, bf16[1,64,3584]{2,1,0:T(8,128)(2,1)S(1)}, u32[]{:S(2)}, u32[]{:S(2)}) %collective-permute-start) | collective-permute-done | bytes 458784 | tf_op jit(solution)/shard_map/ppermute | solution.py:22
  23.3 13.5 %collective-permute-done.1 = bf16[1,64,3584]{2,1,0:T(8,128)(2,1)S(1)} collective-permute-done((bf16[1,64,3584]{2,1,0:T(8,128)(2,1)S(1)}, bf16[1,64,3584]{2,1,0:T(8,128)(2,1)S(1)}, u32[]{:S(2)}, u32[]{:S(2)}) %collective-permute-start.1) | collective-permute-done | bytes 458784 | tf_op jit(solution)/shard_map/ppermute | solution.py:22
  36.8 1.5 pad_maximum_fusion
  38.3 2.5 %collective-permute-start.3 = (s32[1,128]{1,0:T(1,128)S(1)}, s32[1,128]{1,0:T(1,128)S(1)}, u32[]{:S(2)}, u32[]{:S(2)}) collective-permute-start(s32[1,128]{1,0:T(1,128)S(1)} %get-tuple-element.24), channel_id=1, source_target_pairs={{0,2},{2,4},{4,6},{6,8},{8,10},{10,12},{12,14},{14,16},{16,18},{18... | collective-permute-start | bytes 1544 | tf_op jit(solution)/shard_map/ppermute | solution.py:22
  40.9 1.3 collective-permute-start.4
  42.2 1.8 %collective-permute-done.3 = s32[1,128]{1,0:T(1,128)S(1)} collective-permute-done((s32[1,128]{1,0:T(1,128)S(1)}, s32[1,128]{1,0:T(1,128)S(1)}, u32[]{:S(2)}, u32[]{:S(2)}) %collective-permute-start.3) | collective-permute-done | bytes 544 | tf_op jit(solution)/shard_map/ppermute | solution.py:22
  44.1 1.6 collective-permute-done.5
  45.6 1.5 collective-permute-done.4
  50.0 40.4 %all-gather.2.cloned.1.call-done = bf16[1,4,128,3584]{3,2,1,0:T(8,128)(2,1)} async-done(((bf16[1,4,64,3584]{3,2,1,0:T(8,128)(2,1)}), bf16[1,4,128,3584]{3,2,1,0:T(8,128)(2,1)}) %all-gather.2.cloned.1.call-update) | async-done | bytes 3670032 | tf_op jit(solution)/shard_map/all_gather | solution.py:91
  90.3 13.2 %fusion.1 = f32[512,2304]{1,0:T(8,128)S(1)} fusion(bf16[512,3584]{1,0:T(8,128)(2,1)} %bitcast.92, bf16[3584,256]{1,0:T(8,128)(2,1)S(1)} %copy-done.3, bf16[3584,256]{1,0:T(8,128)(2,1)} %param.8, bf16[3584,1792]{1,0:T(8,128)(2,1)} %param.7), kind=kOutput, calls=%fused_computation.1 | convolution fusion | flops 8505262080 | bytes 24903680 | tf_op jit(solution)/shard_map/dot_general | solution.py:94
  103.6 2.0 %slice.65 = f32[512,1792]{1,0:T(8,128)} slice(f32[512,2304]{1,0:T(8,128)S(1)} %fusion.1), slice={[0:512], [0:1792]} | slice | bytes 7340032 | tf_op jit(solution)/shard_map/slice | solution.py:97
  106.5 5.1 %copy.37 = f32[512,1792]{0,1:T(8,128)} copy(f32[512,1792]{1,0:T(8,128)} %slice.65) | data formatting | bytes 7340032 | tf_op jit(solution)/shard_map/slice | solution.py:97
  111.6 3.6 %subtract_convert_fusion = (bf16[512,14,64]{0,2,1:T(8,128)(2,1)}, bf16[512,14,64]{0,2,1:T(8,128)(2,1)S(1)}) fusion(f32[512,14,128]{0,2,1:T(8,128)} %bitcast.76, f32[512,64]{0,1:T(8,128)S(1)} %get-tuple-element.21, f32[512,64]{0,1:T(8,128)S(1)} %get-tuple-element.20), kind=kLoop, calls=%fused_computation.24 | loop fusion | flops 3670016 | bytes 5767168 | tf_op jit(solution)/shard_map/convert.3
  115.5 1.4 fusion.33
  116.9 1.9 %copy.38 = bf16[512,14,64]{2,0,1:T(8,128)(2,1)S(1)} copy(bf16[512,14,64]{0,2,1:T(8,128)(2,1)} %get-tuple-element.8) | data formatting | bytes 1835008 | tf_op jit(solution)/shard_map/convert.3
  118.8 1.6 copy.39
  120.4 1.2 subtract_convert_fusion.1
  121.7 8.9 %fusion.15 = f32[2,512,512,7]{2,1,3,0:T(8,128)} fusion(bf16[512,2,7,64]{3,0,2,1:T(8,128)(2,1)} %bitcast.78, bf16[512,2,7,64]{3,0,2,1:T(8,128)(2,1)S(1)} %bitcast.77, bf16[512,2,64]{2,0,1:T(8,128)(2,1)S(1)} %get-tuple-element.17, bf16[512,2,64]{2,0,1:T(8,128)(2,1)S(1)} %get-tuple-element.16), kind=kOutput, calls=%fused_computation.18 | convolution fusion | flops 943718400 | bytes 16777216 | tf_op jit(solution)/shard_map/qcgd,kcd->cgqk/dot_general | solution.py:54
  130.6 13.6 %fusion.35 = (f32[2,7,512]{2,1,0:T(8,128)S(1)}, bf16[2,7,512,512]{2,3,1,0:T(8,128)(2,1)S(1)}) fusion(f32[2,512,512,7]{2,1,3,0:T(8,128)} %fusion.15, pred[512,512]{0,1:T(8,128)(4,1)S(1)} %copy-done), kind=kOutput, calls=%fused_computation.69 | output fusion | flops 29360640 | bytes 22310912 | tf_op jit(solution)/shard_map/sub | solution.py:67
  146.3 24.7 %all_to_all.5 = bf16[2,1,256,1792]{2,3,1,0:T(8,128)(2,1)S(1)} all-to-all(bf16[2,1,256,1792]{2,3,1,0:T(8,128)(2,1)S(1)} %pad_maximum_fusion.1), channel_id=1, replica_groups=mesh['dp'=16,'sp'=2] {'sp'}, dimensions={0} | all-to-all | bytes 3670016 | tf_op jit(solution)/shard_map/all_to_all | solution.py:15
  170.9 2.5 %copy.47 = bf16[1,256,3584]{2,1,0:T(8,128)(2,1)} copy(bf16[1,256,3584]{1,2,0:T(8,128)(2,1)S(1)} %bitcast.79) | data formatting | bytes 3670016 | tf_op jit(solution)/shard_map/reshape | solution.py:16
  (35 shorter events, 7.4 us)
Async XLA Ops:
  6.5 83.8 %all-gather.2.cloned.1.call-start = ((), (), s32[]{:S(2)}) async-start(), calls=%async_computation.1 | async-start | bytes 5505024 | tf_op jit(solution)/shard_map/all_gather | solution.py:91
  8.1 30.2 %copy-start.2 = (s32[1,4,128]{2,1,0:T(4,128)S(1)}, s32[1,4,128]{2,1,0:T(4,128)}, u32[]{:S(2)}) copy-start(s32[1,4,128]{2,1,0:T(4,128)} %param.6) | copy-start | bytes 6148
  8.1 82.2 %copy-start.3 = (bf16[3584,256]{1,0:T(8,128)(2,1)S(1)}, bf16[3584,256]{1,0:T(8,128)(2,1)}, u32[]{:S(2)}) copy-start(bf16[3584,256]{1,0:T(8,128)(2,1)} %param.9) | copy-start | bytes 5505028
  8.1 14.3 %collective-permute-start = (bf16[1,64,3584]{2,1,0:T(8,128)(2,1)S(1)}, bf16[1,64,3584]{2,1,0:T(8,128)(2,1)S(1)}, u32[]{:S(2)}, u32[]{:S(2)}) collective-permute-start(bf16[1,64,3584]{2,1,0:T(8,128)(2,1)S(1)} %get-tuple-element.13), channel_id=1, source_target_pairs={{0,2},{2,4},{4,6},{6,8},{8,10},{10,12},{12,14},{14,16},{16,18},{18... | collective-permute-start | bytes 1376264 | tf_op jit(solution)/shard_map/ppermute | solution.py:22
  8.7 14.7 %collective-permute-start.2 = (bf16[1,64,3584]{2,1,0:T(8,128)(2,1)S(1)}, bf16[1,64,3584]{2,1,0:T(8,128)(2,1)S(1)}, u32[]{:S(2)}, u32[]{:S(2)}) collective-permute-start(bf16[1,64,3584]{2,1,0:T(8,128)(2,1)S(1)} %get-tuple-element.14), channel_id=1, source_target_pairs={{0,6},{2,8},{4,10},{6,12},{8,14},{10,16},{12,18},{14,20},{16,22},{... | collective-permute-start | bytes 1376264 | tf_op jit(solution)/shard_map/ppermute | solution.py:22
  12.4 24.4 %collective-permute-start.1 = (bf16[1,64,3584]{2,1,0:T(8,128)(2,1)S(1)}, bf16[1,64,3584]{2,1,0:T(8,128)(2,1)S(1)}, u32[]{:S(2)}, u32[]{:S(2)}) collective-permute-start(bf16[1,64,3584]{2,1,0:T(8,128)(2,1)S(1)} %get-tuple-element.15), channel_id=1, source_target_pairs={{0,4},{2,6},{4,8},{6,10},{8,12},{10,14},{12,16},{14,18},{16,20},{1... | collective-permute-start | bytes 1376264 | tf_op jit(solution)/shard_map/ppermute | solution.py:22
  38.3 5.7 %collective-permute-start.3 = (s32[1,128]{1,0:T(1,128)S(1)}, s32[1,128]{1,0:T(1,128)S(1)}, u32[]{:S(2)}, u32[]{:S(2)}) collective-permute-start(s32[1,128]{1,0:T(1,128)S(1)} %get-tuple-element.24), channel_id=1, source_target_pairs={{0,2},{2,4},{4,6},{6,8},{8,10},{10,12},{12,14},{14,16},{16,18},{18... | collective-permute-start | bytes 1544 | tf_op jit(solution)/shard_map/ppermute | solution.py:22
  40.8 4.8 %collective-permute-start.5 = (s32[1,128]{1,0:T(1,128)S(1)}, s32[1,128]{1,0:T(1,128)S(1)}, u32[]{:S(2)}, u32[]{:S(2)}) collective-permute-start(s32[1,128]{1,0:T(1,128)S(1)} %get-tuple-element.25), channel_id=1, source_target_pairs={{0,6},{2,8},{4,10},{6,12},{8,14},{10,16},{12,18},{14,20},{16,22},{... | collective-permute-start | bytes 1544 | tf_op jit(solution)/shard_map/ppermute | solution.py:22
  40.9 6.3 %collective-permute-start.4 = (s32[1,128]{1,0:T(1,128)S(1)}, s32[1,128]{1,0:T(1,128)S(1)}, u32[]{:S(2)}, u32[]{:S(2)}) collective-permute-start(s32[1,128]{1,0:T(1,128)S(1)} %get-tuple-element.26), channel_id=1, source_target_pairs={{0,4},{2,6},{4,8},{6,10},{8,12},{10,14},{12,16},{14,18},{16,20},{1... | collective-permute-start | bytes 1544 | tf_op jit(solution)/shard_map/ppermute | solution.py:22
  121.7 8.9 %copy-start = (pred[512,512]{0,1:T(8,128)(4,1)S(1)}, pred[512,512]{0,1:T(8,128)(4,1)}, u32[]{:S(2)}) copy-start(pred[512,512]{0,1:T(8,128)(4,1)} %fusion.20) | copy-start | bytes 786436
  130.6 13.7 %copy-start.1 = (bf16[512,256]{0,1:T(8,128)(2,1)S(1)}, bf16[512,256]{0,1:T(8,128)(2,1)}, u32[]{:S(2)}) copy-start(bf16[512,256]{0,1:T(8,128)(2,1)} %copy.46) | copy-start | bytes 786436
Sparse Core Ops, SparseCore 0:
  38.4 51.8 all-gather.1
